TPU v7x, 128 devices: a whole 4x4x4 slice. The times are simulated.
128 devices in a mesh: dp: 128 (over z, y, x, core).
Axes of the slice: x: 4, y: 4, z: 4, core: 2. Of those that a mesh axis runs over, the one named last changes fastest.
Arguments:
- attended: bfloat16 [65536, 1152], P('dp'), may hold values from -24 to 24, as said below
- proj_cot: bfloat16 [65536, 1152], P('dp'), may hold values from -0.00036621094 to 0.00036621094
- timesteps: float32 [256], P('dp'), may hold values from 0 to 1
- embed_cot: bfloat16 [256, 1152], P('dp'), may hold values from -0.015625 to 0.015625
- master_proj: float32 [1327104], P('dp'), may hold values from -0.1875 to 0.1875
- moment_proj: float32 [1327104], P('dp'), may hold values from -0.013671875 to 0.013671875
- second_proj: float32 [1327104], P('dp'), may hold values from 1.8838011e-07 to 3.0140818e-06
- master_embed: float32 [294912], P('dp'), may hold values from -0.375 to 0.375
- moment_embed: float32 [294912], P('dp'), may hold values from -0.02734375 to 0.02734375
- squared_moment_layer: float32 [294912], P('dp'), may hold values from 8.477105e-07 to 1.3563368e-05
- attended_next: bfloat16 [65536, 1152], P('dp'), may hold values from -6 to 6
- timesteps_next: float32 [256], P('dp'), may hold values from 0 to 1
Outputs:
- next_proj: bfloat16 [65536, 1152], P('dp')
- next_embed: bfloat16 [256, 1152], P('dp')
- move_direction_output: float32 [1327104], P('dp')
- step_embed: float32 [294912], P('dp')
- master_proj_new: float32 [1327104], P('dp')
- master_embed_new: float32 [294912], P('dp')
- grad_norm: float32 [], replicated
Inputs may be any that keep to these rules, and one draw needn't show every extreme that they name: attended has entries of mean zero whose scale differs between feature columns by up to a factor of 16.
All inputs are finite; a program needn't handle non-finite values.
Results may differ from a plain program's by a relative error of at most 0.0025.
Values may be sent and summed in bfloat16 or wider, within the bound.
A program may use at most 64 MiB of HBM per device.

v0:
```python
import math
import jax
import jax.numpy as jnp
from jax import lax
from jax.sharding import Mesh
from jax.sharding import PartitionSpec as P

DP = ("dp_0", "dp_1", "dp_2", "dp_3")
beta_one = 0.9
beta_two = 0.999
step_count = 1000.0
learn_rate = 0.0001
shrink_factor = 0.01
epsilon = 1e-08
max_norm = 1.0


def over_axes(value, axes):
    for axis in axes:
        value = lax.psum(value, axis)
    return value


def joined_along(blocks, dim):
    lengths = list(blocks.shape[1:])
    lengths[dim] *= blocks.shape[0]
    return jnp.moveaxis(blocks, 0, dim).reshape(lengths)


def gather_packed(arrays, axis, dims):
    flat = jnp.concatenate([a.reshape(-1) for a in arrays])
    lines, at, finished = (lax.all_gather(flat, axis), 0, [])
    for a, dim in zip(arrays, dims):
        blocks = lines[:, at : at + a.size].reshape(-1, *a.shape)
        finished.append(joined_along(blocks, dim))
        at += a.size
    return tuple(finished)


def freq_embed(moments, width):
    half_width = width // 2
    ladder = jnp.arange(half_width, dtype=jnp.float32)
    freqs = jnp.exp(-math.log(10000.0) * ladder / half_width)
    phase_values = (moments * 1000.0)[:, None] * freqs[None, :]
    return jnp.concatenate([jnp.cos(phase_values), jnp.sin(phase_values)], axis=1).astype(
        jnp.bfloat16
    )


def adamw_update(gradient, clip, master, moment, second):
    scaled = clip * gradient
    first_new = beta_one * moment + (1.0 - beta_one) * scaled
    second_new = beta_two * second + (1.0 - beta_two) * scaled * scaled
    first_hat = first_new / (1.0 - beta_one**step_count)
    second_hat = second_new / (1.0 - beta_two**step_count)
    direction = first_hat / (jnp.sqrt(second_hat) + epsilon)
    freshened_values = master - learn_rate * (direction + shrink_factor * master)
    return (direction, freshened_values)


def shards(
    attended,
    proj_cot,
    timesteps,
    embed_cot,
    master_proj,
    moment_proj,
    second_proj,
    master_embed,
    moment_embed,
    squared_moment_layer,
    attended_next,
    timesteps_next,
):
    width = attended.shape[1]
    freq_width = master_embed.shape[0] * lax.axis_size(DP) // width
    term_proj = jnp.dot(attended.T, proj_cot, preferred_element_type=jnp.float32).reshape(-1)
    freq_now = freq_embed(timesteps, freq_width)
    term_embed = jnp.dot(freq_now.T, embed_cot, preferred_element_type=jnp.float32).reshape(-1)
    grad_proj, grad_embed = (
        lax.psum_scatter(term_proj, DP, scatter_dimension=0, tiled=True),
        lax.psum_scatter(term_embed, DP, scatter_dimension=0, tiled=True),
    )
    square_proj = over_axes(jnp.sum(grad_proj * grad_proj), DP)
    square_embed = over_axes(jnp.sum(grad_embed * grad_embed), DP)
    total = square_proj + square_embed
    grad_norm = jnp.sqrt(total)
    clip = jnp.minimum(jnp.float32(1.0), max_norm / (grad_norm + 1e-06))
    move_direction_output, master_proj_new = adamw_update(
        grad_proj, clip, master_proj, moment_proj, second_proj
    )
    step_embed, master_embed_new = adamw_update(
        grad_embed, clip, master_embed, moment_embed, squared_moment_layer
    )
    shard_proj = master_proj_new.astype(jnp.bfloat16)
    shard_embed = master_embed_new.astype(jnp.bfloat16)
    whole_proj, whole_embed = gather_packed((shard_proj, shard_embed), DP, (0, 0))
    weight_proj = whole_proj.reshape(width, width)
    weight_embed = whole_embed.reshape(freq_width, width)
    next_proj = jnp.dot(attended_next, weight_proj, preferred_element_type=jnp.float32).astype(
        jnp.bfloat16
    )
    freq_next = freq_embed(timesteps_next, freq_width)
    next_embed = jnp.dot(freq_next, weight_embed, preferred_element_type=jnp.float32).astype(
        jnp.bfloat16
    )
    return (
        next_proj,
        next_embed,
        move_direction_output,
        step_embed,
        master_proj_new,
        master_embed_new,
        grad_norm,
    )


def solution(mesh):
    finer = Mesh(mesh.devices.reshape(4, 4, 4, 2), ("dp_0", "dp_1", "dp_2", "dp_3"))
    return jax.shard_map(
        shards,
        mesh=finer,
        in_specs=(
            P(DP, None),
            P(DP, None),
            P(DP),
            P(DP, None),
            P(DP),
            P(DP),
            P(DP),
            P(DP),
            P(DP),
            P(DP),
            P(DP, None),
            P(DP),
        ),
        out_specs=(P(DP, None), P(DP, None), P(DP), P(DP), P(DP), P(DP), P()),
        check_vma=False,
    )
```

profile of v0, /device:TPU:1, one launch (start us, length us, event | category | flops | bytes accessed | tf_op | source)
XLA Modules:
  0.0 314.4 jit_solution(12199632284855341670)
XLA Ops:
  7.2 0.0 copy-start
  7.2 0.0 all-reduce.5.cloned.1.call-start
  7.2 0.8 broadcast_multiply_fusion
  8.0 0.1 fusion.13
  8.1 1.1 fusion.15
  9.2 0.0 copy-start.1
  9.2 1.1 reshape.28
  10.3 0.0 copy-done
  10.3 0.6 copy-done.1
  10.9 4.1 %fusion.28 = f32[1152,1152]{1,0:T(8,128)} fusion(bf16[512,1152]{1,0:T(8,128)(2,1)S(1)} %copy-done, bf16[512,1152]{1,0:T(8,128)(2,1)S(1)} %copy-done.1), kind=kOutput, calls=%fused_computation.43 | convolution fusion | flops 1358954496 | bytes 7667712 | tf_op jit(solution)/shard_map/dot_general | solution.py:77
  15.0 6.6 %reshape.27 = f32[1327104]{0:T(1024)} reshape(f32[1152,1152]{1,0:T(8,128)} %fusion.28) | data formatting | bytes 10616832 | tf_op jit(solution)/shard_map/reshape | solution.py:77
  21.5 0.0 copy-start.2
  21.5 0.0 copy-start.3
  21.5 0.0 copy-start.4
  21.5 0.0 copy-start.5
  21.5 0.0 copy-start.6
  21.5 0.0 copy-start.7
  21.5 0.0 all-reduce.5.cloned.1.call-update
  21.6 0.0 all-gather.4.cloned.1.call-start
  21.6 161.1 %all-reduce.5.cloned.1.call-done = (f32[294912]{0:T(1024)}, f32[1327104]{0:T(1024)}) async-done(((f32[294912]{0:T(1024)}, f32[1327104]{0:T(1024)}), (f32[294912]{0:T(1024)}, f32[1327104]{0:T(1024)})) %all-reduce.5.cloned.1.call-update) | async-done | bytes 6488080
  182.8 1.5 multiply_reduce_fusion
  184.2 1.4 multiply_reduce_fusion.1
  186.9 9.0 %psum.67 = f32[]{:T(128)} all-reduce(f32[]{:T(128)S(6)} %add.56), channel_id=1, replica_groups=mesh['dp_0'=4,'dp_1'=4,'dp_2'=4,'dp_3'=2] {'dp_0'}, use_global_device_ids=true, to_apply=%region_2.0 | all-reduce | flops 1 | bytes 8 | tf_op jit(solution)/shard_map/psum | solution.py:20
  195.9 7.8 %psum.66 = f32[]{:T(128)} all-reduce(f32[]{:T(128)} %psum.67), channel_id=1, replica_groups=mesh['dp_0'=4,'dp_1'=4,'dp_2'=4,'dp_3'=2] {'dp_1'}, use_global_device_ids=true, to_apply=%region_3.0 | all-reduce | flops 1 | bytes 8 | tf_op jit(solution)/shard_map/psum | solution.py:20
  203.7 7.8 %psum.65 = f32[]{:T(128)} all-reduce(f32[]{:T(128)} %psum.66), channel_id=1, replica_groups=mesh['dp_0'=4,'dp_1'=4,'dp_2'=4,'dp_3'=2] {'dp_2'}, use_global_device_ids=true, to_apply=%region_4.0 | all-reduce | flops 1 | bytes 8 | tf_op jit(solution)/shard_map/psum | solution.py:20
  211.5 9.2 %psum.64 = f32[]{:T(128)} all-reduce(f32[]{:T(128)} %psum.65), channel_id=1, replica_groups=mesh['dp_0'=4,'dp_1'=4,'dp_2'=4,'dp_3'=2] {'dp_3'}, use_global_device_ids=true, to_apply=%region_5.0 | all-reduce | flops 1 | bytes 8 | tf_op jit(solution)/shard_map/psum | solution.py:20
  221.5 0.0 copy-done.2
  221.5 0.0 copy-done.3
  221.5 0.0 copy-done.4
  221.5 1.6 fusion.24
  223.1 0.0 copy-done.5
  223.1 0.0 copy-done.6
  223.1 0.0 copy-done.7
  223.1 1.4 fusion.26
  224.5 0.6 reshape.30
  225.2 0.0 all-gather.4.cloned.1.call-update
  225.2 63.7 %all-gather.4.cloned.1.call-done = bf16[128,1,12672]{2,1,0:T(2,128)(2,1)} async-done(((bf16[1,1,12672]{2,1,0:T(2,128)(2,1)}), bf16[128,1,12672]{2,1,0:T(2,128)(2,1)}) %all-gather.4.cloned.1.call-update) | async-done | bytes 3244048 | tf_op jit(solution)/shard_map/all_gather | solution.py:32
  288.9 3.2 %copy.24 = bf16[128,1,12672]{2,0,1:T(8,128)(2,1)S(1)} copy(bf16[128,1,12672]{2,1,0:T(2,128)(2,1)} %all-gather.4.cloned.1.call-done) | data formatting | bytes 6488064
  292.1 1.7 slice.8
  293.9 6.4 %reshape_reshape.6 = bf16[1152,1152]{1,0:T(8,128)(2,1)} reshape(bf16[128,10368]{1,0:T(8,128)(2,1)} %slice.8) | data formatting | bytes 5308416 | tf_op jit(solution)/shard_map/reshape;reshape | solution.py:98
  300.2 3.8 %fusion = bf16[512,1152]{0,1:T(8,128)(2,1)S(1)} fusion(bf16[1152,1152]{1,0:T(8,128)(2,1)} %reshape_reshape.6, bf16[512,1152]{1,0:T(8,128)(2,1)} %param.22), kind=kOutput, calls=%fused_computation.2 | convolution fusion | flops 1359544320 | bytes 5013504 | tf_op jit(solution)/shard_map/dot_general | solution.py:100
  304.0 1.4 copy.21
  305.5 0.2 reshape_reshape.7
  305.7 0.8 convolution_convert_fusion.1
  (3 shorter events, 0.1 us)
Async XLA Ops:
  7.2 3.1 copy-start
  7.2 175.6 %all-reduce.5.cloned.1.call-start = ((), (), s32[]{:S(2)}) async-start(), calls=%async_computation.1 | async-start | bytes 12976128
  9.2 1.7 copy-start.1
  21.5 200.0 %copy-start.2 = (f32[10368]{0:T(1024)S(1)}, f32[10368]{0:T(1024)}, u32[]{:S(2)}) copy-start(f32[10368]{0:T(1024)} %param.16) | copy-start | bytes 124420
  21.5 200.0 %copy-start.3 = (f32[10368]{0:T(1024)S(1)}, f32[10368]{0:T(1024)}, u32[]{:S(2)}) copy-start(f32[10368]{0:T(1024)} %param.18) | copy-start | bytes 124420
  21.5 200.0 %copy-start.4 = (f32[10368]{0:T(1024)S(1)}, f32[10368]{0:T(1024)}, u32[]{:S(2)}) copy-start(f32[10368]{0:T(1024)} %param.17) | copy-start | bytes 124420
  21.5 201.6 %copy-start.5 = (f32[2304]{0:T(1024)S(1)}, f32[2304]{0:T(1024)}, u32[]{:S(2)}) copy-start(f32[2304]{0:T(1024)} %param.19) | copy-start | bytes 27652
  21.5 201.6 %copy-start.6 = (f32[2304]{0:T(1024)S(1)}, f32[2304]{0:T(1024)}, u32[]{:S(2)}) copy-start(f32[2304]{0:T(1024)} %param.21) | copy-start | bytes 27652
  21.5 201.6 %copy-start.7 = (f32[2304]{0:T(1024)S(1)}, f32[2304]{0:T(1024)}, u32[]{:S(2)}) copy-start(f32[2304]{0:T(1024)} %param.20) | copy-start | bytes 27652
  21.6 267.4 %all-gather.4.cloned.1.call-start = ((), (), s32[]{:S(2)}) async-start(), calls=%async_computation | async-start | bytes 6538752 | tf_op jit(solution)/shard_map/all_gather | solution.py:32
Sparse Core Ops, SparseCore 0:
  21.7 161.0 all-reduce.4
  225.3 63.5 all-gather.3
where the time goes:
time: 315 us; the launch traced here: 314 us
  waiting for transfers between devices  225 us (71%)
  blocking collectives  33.8 us (11%)
  local copies, waits for them, and re-layouts  21.8 us (7%)
  between operations  17.3 us (5%)
  matrix products  9.73 us (3%)
  other arithmetic  6.77 us (2%)
    unnamed x3, waiting for transfers between devices  161 us
    all_gather x1, waiting for transfers between devices, gather_packed(): lines, at, finished = (lax.all_gather(flat, axis), 0, [])  63.7 us
    psum x4, blocking collectives, over_axes(): value = lax.psum(value, axis)  33.8 us
    reshape x1, local copies, waits for them, and re-layouts, shards(): jnp.dot(attended.T, proj_cot, preferred_element_type=jnp.float32)  6.55 us
    another operation x1, local copies, waits for them, and re-layouts, shards(): weight_proj = whole_proj.reshape(width, width)  6.36 us
  transfers between devices with their start and end apart: 2, of which 2 were waited for; matrix products, arithmetic and copies ran while one was open for 0% of the time, Pallas kernels for 0%

commit v1 on v0

--- a/solution.py
+++ b/solution.py
@@ -17,7 +17,7 @@
 
 def over_axes(value, axes):
     for axis in axes:
-        value = lax.psum(value, axis)
+        value = jnp.sum(jax.lax.all_gather(value, axis), 0)
     return value
 
 

time: 315 us -> 330 us (1.048)
  local copies, waits for them, and re-layouts: 21.8 us -> 35.9 us
  other arithmetic: 6.77 us -> 11.6 us
    psum x4 -> x0, blocking collectives: 33.8 us -> none  [over_axes(): value = lax.psum(value, axis)]
    unnamed x0 -> x4, blocking collectives: none -> 31.4 us
    unnamed x19 -> x47, local copies, waits for them, and re-layouts: 5.88 us -> 19.9 us
    reduce_sum x0 -> x8, other arithmetic: none -> 4.81 us  [over_axes(): value = jnp.sum(jax.lax.all_gather(value, axis), 0)]
where the time goes in v1:
time: 330 us; the launch traced here: 329 us
  waiting for transfers between devices  224 us (68%)
  local copies, waits for them, and re-layouts  35.9 us (11%)
  blocking collectives  31.4 us (10%)
  between operations  16.7 us (5%)
  other arithmetic  11.6 us (4%)
  matrix products  9.73 us (3%)
    unnamed x3, waiting for transfers between devices  160 us
    all_gather x1, waiting for transfers between devices, gather_packed(): lines, at, finished = (lax.all_gather(flat, axis), 0, [])  63.7 us
    unnamed x4, blocking collectives  31.4 us
    unnamed x47, local copies, waits for them, and re-layouts  19.9 us
  transfers between devices with their start and end apart: 2, of which 2 were waited for; matrix products, arithmetic and copies ran while one was open for 0% of the time, Pallas kernels for 0%

profile of v1, /device:TPU:1, one launch (start us, length us, event | category | flops | bytes accessed | tf_op | source)
XLA Modules:
  0.0 329.2 jit_solution(6638782126000948072)
XLA Ops:
  7.2 0.0 all-reduce.17.cloned.1.call-start
  7.2 0.8 broadcast_multiply_fusion
  8.0 0.1 fusion.13
  8.1 1.1 fusion.15
  9.2 1.1 reshape.28
  10.3 0.6 copy-done.1
  10.9 4.1 %fusion.28 = f32[1152,1152]{1,0:T(8,128)} fusion(bf16[512,1152]{1,0:T(8,128)(2,1)S(1)} %copy-done, bf16[512,1152]{1,0:T(8,128)(2,1)S(1)} %copy-done.1), kind=kOutput, calls=%fused_computation.43 | convolution fusion | flops 1358954496 | bytes 7667712 | tf_op jit(solution)/shard_map/dot_general | solution.py:77
  15.0 6.6 %reshape.27 = f32[1327104]{0:T(1024)} reshape(f32[1152,1152]{1,0:T(8,128)} %fusion.28) | data formatting | bytes 10616832 | tf_op jit(solution)/shard_map/reshape | solution.py:77
  21.6 0.0 all-gather.4.cloned.1.call-start
  21.7 0.5 copy-done.11
  22.2 0.6 dynamic-slice
  22.7 160.1 %all-reduce.17.cloned.1.call-done = (f32[294912]{0:T(1024)}, f32[1327104]{0:T(1024)}) async-done(((f32[294912]{0:T(1024)}, f32[1327104]{0:T(1024)}), (f32[294912]{0:T(1024)}, f32[1327104]{0:T(1024)})) %all-reduce.17.cloned.1.call-update) | async-done | bytes 6488080
  182.8 1.5 multiply_reduce_fusion
  184.3 1.4 multiply_reduce_fusion.1
  185.7 1.4 dynamic-update-slice
  187.1 1.4 dynamic-update-slice.4
  188.5 0.6 dynamic-slice.1
  189.1 8.4 %all-reduce.13 = (f32[4]{0:T(128)S(1)}, f32[4]{0:T(128)S(1)}) all-reduce(f32[4]{0:T(128)S(1)} %dynamic-update-slice, f32[4]{0:T(128)S(1)} %dynamic-update-slice.4), channel_id=1, replica_groups=mesh['dp_0'=4,'dp_1'=4,'dp_2'=4,'dp_3'=2] {'dp_0'}, use_global_device_ids=true, to_apply=%add | all-reduce | flops 8 | bytes 64
  197.5 0.6 reduce_sum.96
  198.1 0.6 reduce_sum.91
  198.7 1.4 dynamic-update-slice.5
  200.1 1.4 dynamic-update-slice.1
  201.5 0.6 dynamic-slice.2
  202.1 7.2 %all-reduce.12 = (f32[4]{0:T(128)S(1)}, f32[4]{0:T(128)S(1)}) all-reduce(f32[4]{0:T(128)S(1)} %dynamic-update-slice.1, f32[4]{0:T(128)S(1)} %dynamic-update-slice.5), channel_id=1, replica_groups=mesh['dp_0'=4,'dp_1'=4,'dp_2'=4,'dp_3'=2] {'dp_1'}, use_global_device_ids=true, to_apply=%add.1 | all-reduce | flops 8 | bytes 64
  209.3 0.6 reduce_sum.97
  209.9 0.6 reduce_sum.92
  210.5 1.4 dynamic-update-slice.6
  211.9 1.4 dynamic-update-slice.2
  213.3 0.6 dynamic-slice.3
  213.9 7.2 %all-reduce.11 = (f32[4]{0:T(128)S(1)}, f32[4]{0:T(128)S(1)}) all-reduce(f32[4]{0:T(128)S(1)} %dynamic-update-slice.2, f32[4]{0:T(128)S(1)} %dynamic-update-slice.6), channel_id=1, replica_groups=mesh['dp_0'=4,'dp_1'=4,'dp_2'=4,'dp_3'=2] {'dp_2'}, use_global_device_ids=true, to_apply=%add.2 | all-reduce | flops 8 | bytes 64
  221.1 0.6 reduce_sum.98
  221.7 0.6 reduce_sum.93
  222.3 1.4 dynamic-update-slice.7
  223.7 1.4 dynamic-update-slice.3
  225.1 8.6 %all-reduce.14 = (f32[2]{0:T(128)S(1)}, f32[2]{0:T(128)S(1)}) all-reduce(f32[2]{0:T(128)S(1)} %dynamic-update-slice.3, f32[2]{0:T(128)S(1)} %dynamic-update-slice.7), channel_id=1, replica_groups=mesh['dp_0'=4,'dp_1'=4,'dp_2'=4,'dp_3'=2] {'dp_3'}, use_global_device_ids=true, to_apply=%add.3 | all-reduce | flops 4 | bytes 32
  233.7 0.6 reduce_sum.94
  234.3 0.6 reduce_sum.99
  236.3 1.6 fusion.24
  237.9 1.4 fusion.26
  239.3 0.6 reshape.54
  240.0 63.7 %all-gather.4.cloned.1.call-done = bf16[128,1,12672]{2,1,0:T(2,128)(2,1)} async-done(((bf16[1,1,12672]{2,1,0:T(2,128)(2,1)}), bf16[128,1,12672]{2,1,0:T(2,128)(2,1)}) %all-gather.4.cloned.1.call-update) | async-done | bytes 3244048 | tf_op jit(solution)/shard_map/all_gather | solution.py:32
  303.7 3.2 copy.24
  306.9 1.7 slice.8
  308.6 6.4 %reshape_reshape.6 = bf16[1152,1152]{1,0:T(8,128)(2,1)} reshape(bf16[128,10368]{1,0:T(8,128)(2,1)} %slice.8) | data formatting | bytes 5308416 | tf_op jit(solution)/shard_map/reshape;reshape | solution.py:98
  315.0 3.8 %fusion = bf16[512,1152]{0,1:T(8,128)(2,1)S(1)} fusion(bf16[1152,1152]{1,0:T(8,128)(2,1)} %reshape_reshape.6, bf16[512,1152]{1,0:T(8,128)(2,1)} %param.22), kind=kOutput, calls=%fused_computation.2 | convolution fusion | flops 1359544320 | bytes 5013504 | tf_op jit(solution)/shard_map/dot_general | solution.py:100
  318.8 1.4 copy.21
  320.2 0.2 reshape_reshape.7
  320.4 0.8 convolution_convert_fusion.1
  (35 shorter events, 0.2 us)
Async XLA Ops:
  7.2 3.1 copy-start
  7.2 175.6 %all-reduce.17.cloned.1.call-start = ((), (), s32[]{:S(2)}) async-start(), calls=%async_computation.1 | async-start | bytes 12976128
  9.2 1.7 copy-start.1
  21.5 0.7 copy-start.11
  21.5 167.0 %copy-start.10 = (u32[128]{0:T(128)S(1)}, u32[128]{0:T(128)}, u32[]{:S(2)}) copy-start(u32[128]{0:T(128)} %constant.51) | copy-start | bytes 1540
  21.5 180.0 %copy-start.9 = (u32[128]{0:T(128)S(1)}, u32[128]{0:T(128)}, u32[]{:S(2)}) copy-start(u32[128]{0:T(128)} %constant.56) | copy-start | bytes 1540
  21.5 191.8 %copy-start.8 = (u32[128]{0:T(128)S(1)}, u32[128]{0:T(128)}, u32[]{:S(2)}) copy-start(u32[128]{0:T(128)} %constant.61) | copy-start | bytes 1540
  21.5 214.7 %copy-start.2 = (f32[10368]{0:T(1024)S(1)}, f32[10368]{0:T(1024)}, u32[]{:S(2)}) copy-start(f32[10368]{0:T(1024)} %param.16) | copy-start | bytes 124420
  21.5 214.7 %copy-start.3 = (f32[10368]{0:T(1024)S(1)}, f32[10368]{0:T(1024)}, u32[]{:S(2)}) copy-start(f32[10368]{0:T(1024)} %param.18) | copy-start | bytes 124420
  21.5 214.7 %copy-start.4 = (f32[10368]{0:T(1024)S(1)}, f32[10368]{0:T(1024)}, u32[]{:S(2)}) copy-start(f32[10368]{0:T(1024)} %param.17) | copy-start | bytes 124420
  21.6 216.3 %copy-start.5 = (f32[2304]{0:T(1024)S(1)}, f32[2304]{0:T(1024)}, u32[]{:S(2)}) copy-start(f32[2304]{0:T(1024)} %param.19) | copy-start | bytes 27652
  21.6 216.3 %copy-start.6 = (f32[2304]{0:T(1024)S(1)}, f32[2304]{0:T(1024)}, u32[]{:S(2)}) copy-start(f32[2304]{0:T(1024)} %param.21) | copy-start | bytes 27652
  21.6 216.3 %copy-start.7 = (f32[2304]{0:T(1024)S(1)}, f32[2304]{0:T(1024)}, u32[]{:S(2)}) copy-start(f32[2304]{0:T(1024)} %param.20) | copy-start | bytes 27652
  21.6 282.1 %all-gather.4.cloned.1.call-start = ((), (), s32[]{:S(2)}) async-start(), calls=%async_computation | async-start | bytes 6538752 | tf_op jit(solution)/shard_map/all_gather | solution.py:32
Sparse Core Ops, SparseCore 0:
  21.7 161.0 all-reduce.16
  240.1 63.5 all-gather.3
